TPU v7x, 32 devices: a whole 2x2x4 slice. The times are simulated.
32 devices in a mesh: ta: 2 (over x), gz: 4 (over z), xy: 4 (over y, core).
Axes of the slice: x: 2, y: 2, z: 4, core: 2. Of those that a mesh axis runs over, the one named last changes fastest.
Arguments:
- source: float32 [2, 48, 2, 4, 512], P(None, None, 'ta', 'gz', 'xy'), may hold values from -14 to 14
- inverse: bfloat16 [2, 48, 48, 2, 4, 512], P(None, None, None, 'ta', 'gz', 'xy'), may hold values from -0.625 to 0.625
- coarse_links: bfloat16 [8, 2, 48, 48, 2, 4, 512], P(None, None, None, None, 'ta', 'gz', 'xy'), may hold values from -0.15625 to 0.15625
Outputs:
- solution: float32 [2, 48, 2, 4, 512], P(None, None, 'ta', 'gz', 'xy')
- residual: float32 [2, 48, 2, 4, 512], P(None, None, 'ta', 'gz', 'xy')
- hessenberg: float32 [2, 6, 5], replicated
All inputs are finite; a program needn't handle non-finite values.
Results may differ from a plain program's by a relative error of at most 0.0003.
Values sent between devices are 32-bit elements; how exact they have to be, the bound alone decides.
A program may use at most 128 MiB of HBM per device.

v0:
```python
import functools

import jax
import jax.numpy as jnp
from jax import lax
from jax.experimental import pallas as pl
from jax.experimental.pallas import tpu as pltpu
from jax.sharding import PartitionSpec as P

LY = 16
ITERS = 5
SUB = 8
MESH = pl.DeviceIdType.MESH
ARRIVAL = (6, 7, 4, 5, 0, 1, 2, 3)


def cmul(a, b):
    return (a[0] * b[0] - a[1] * b[1], a[0] * b[1] + a[1] * b[0])


def cmul_conj(a, b):
    return (a[0] * b[0] + a[1] * b[1], a[0] * b[1] - a[1] * b[0])


def csub(a, b):
    return (a[0] - b[0], a[1] - b[1])


def cscale(a, s):
    return (a[0] * s, a[1] * s)


def kernel(sizes, source_hbm, inverse_hbm, links_hbm, sol_ref, res_ref, hes_ref,
           stage, mat_a, mat_b, mat_s, vecs, acc, src, fields, vs, qs,
           halo_t, halo_z, halo_x, pack, red_one, red_two, row_one, row_two,
           load_sem, src_sem, t_send, t_recv, z_send, z_recv, x_send, x_recv,
           one_send, one_recv, two_send, two_recv):
    n_ta, n_gz, n_xy = sizes
    comp, lanes = src.shape[1], src.shape[2]
    tiles = comp // SUB
    me_ta, me_gz, me_xy = (lax.axis_index(a) for a in ("ta", "gz", "xy"))
    n_two = n_ta * n_gz
    me_two = me_ta * n_gz + me_gz

    pltpu.make_async_copy(source_hbm, src, src_sem).start()
    loads = []
    for d in ARRIVAL:
        loads.append(pltpu.make_async_copy(links_hbm.at[d], stage.at[d], load_sem.at[d]))
    loads.append(pltpu.make_async_copy(inverse_hbm, stage.at[8], load_sem.at[8]))
    for load in loads:
        load.start()

    def two_peer(k):
        p = lax.rem(me_two + k, n_two)
        return p, {"ta": p // n_gz, "gz": lax.rem(p, n_gz)}

    barrier = pltpu.get_barrier_semaphore()
    for k in range(1, n_xy):
        pl.semaphore_signal(barrier, inc=1, device_id={"xy": lax.rem(me_xy + k, n_xy)}, device_id_type=MESH)
    for k in range(1, n_two):
        pl.semaphore_signal(barrier, inc=1, device_id=two_peer(k)[1], device_id_type=MESH)
    pltpu.make_async_copy(source_hbm, src, src_sem).wait()
    pl.semaphore_wait(barrier, n_xy - 1 + n_two - 1)

    lane = lax.broadcasted_iota(jnp.int32, (SUB, lanes), 1)
    lane_all = lax.broadcasted_iota(jnp.int32, (comp, lanes), 1)
    pending = []

    def remote(s, d, send, recv, device):
        return pltpu.make_async_remote_copy(
            src_ref=s, dst_ref=d, send_sem=send, recv_sem=recv, device_id=device, device_id_type=MESH)

    def packed(value, first):
        out = jnp.zeros((SUB, lanes), jnp.float32)
        for k in range(tiles):
            tile = value[k * SUB:(k + 1) * SUB]
            shift = (LY * k + (0 if first else LY)) % lanes
            if shift:
                tile = pltpu.roll(tile, shift, 1)
            out = jnp.where(lane // LY == k, tile, out)
        return out

    def unpacked(value, first):
        out = []
        for k in range(tiles):
            shift = ((0 if first else lanes - LY) - LY * k) % lanes
            out.append(pltpu.roll(value, shift, 1) if shift else value)
        return jnp.concatenate(out, axis=0)

    def send_halo(e, ref):
        for c in range(2):
            value = ref[c]
            pack[e, 0, c] = packed(value, True)
            pack[e, 1, c] = packed(value, False)
        waits = {}
        for slot, step in ((0, n_xy - 1), (1, 1)):
            cp = remote(pack.at[e, slot], halo_x.at[e, slot], x_send.at[e, slot], x_recv.at[e, slot],
                        {"xy": lax.rem(me_xy + step, n_xy)})
            cp.start()
            pending.append(cp)
            waits["x", slot] = cp
        for slot, step in ((0, n_gz - 1), (1, 1)):
            cp = remote(ref, halo_z.at[e, slot], z_send.at[e, slot], z_recv.at[e, slot],
                        {"gz": lax.rem(me_gz + step, n_gz)})
            cp.start()
            pending.append(cp)
            waits["z", slot] = cp
        for slot, step in ((0, n_ta - 1), (1, 1))[:1 if n_ta == 2 else 2]:
            cp = remote(ref, halo_t.at[e, slot], t_send.at[e, slot], t_recv.at[e, slot],
                        {"ta": lax.rem(me_ta + step, n_ta)})
            cp.start()
            pending.append(cp)
            waits["t", slot] = cp
        return waits

    def put(slot, re, im):
        vecs[slot, 0] = re
        vecs[slot, 1] = im - re
        vecs[slot, 2] = re + im

    def set_y(ref):
        pos = lane_all % LY
        fwd, bwd = [], []
        for c in range(2):
            v = ref[c]
            fwd.append(jnp.where(pos == LY - 1, pltpu.roll(v, LY - 1, 1), pltpu.roll(v, lanes - 1, 1)))
            bwd.append(jnp.where(pos == 0, pltpu.roll(v, lanes - LY + 1, 1), pltpu.roll(v, 1, 1)))
        put(6, *fwd)
        put(7, *bwd)

    def set_x(e, ref, waits):
        fwd, bwd = [], []
        waits["x", 0].wait_recv()
        waits["x", 1].wait_recv()
        for c in range(2):
            v = ref[c]
            fwd.append(jnp.where(lane_all >= lanes - LY, unpacked(halo_x[e, 0, c], False), pltpu.roll(v, lanes - LY, 1)))
            bwd.append(jnp.where(lane_all < LY, unpacked(halo_x[e, 1, c], True), pltpu.roll(v, LY, 1)))
        put(4, *fwd)
        put(5, *bwd)

    def set_t(e, waits):
        waits["t", 0].wait_recv()
        put(0, halo_t[e, 0, 0], halo_t[e, 0, 1])
        back = 0
        if n_ta != 2:
            waits["t", 1].wait_recv()
            back = 1
        put(1, halo_t[e, back, 0], halo_t[e, back, 1])

    def set_z(e, waits):
        for slot in range(2):
            waits["z", slot].wait_recv()
            put(2 + slot, halo_z[e, slot, 0], halo_z[e, slot, 1])

    def convert(d):
        def body(i, _):
            rows = pl.ds(i * 2, 2)
            a = stage[d, 0, rows].astype(jnp.float32)
            b = stage[d, 1, rows].astype(jnp.float32)
            mat_a[d, rows] = a
            mat_b[d, rows] = b
            mat_s[d, rows] = a + b
            return 0

        lax.fori_loop(0, comp // 2, body, 0)

    def products(dirs, first, out=None):
        def body(b, _):
            rows = pl.ds(b * SUB, SUB)
            if first:
                sums = [jnp.zeros((SUB, SUB, lanes), jnp.float32)] * 3
            else:
                sums = [acc[m, rows] for m in range(3)]
            for d in dirs:
                slot = 0 if d == 8 else d
                for k in range(tiles):
                    cols = pl.ds(k * SUB, SUB)
                    for m, mat in enumerate((mat_s, mat_a, mat_b)):
                        sums[m] = sums[m] + mat[d, rows, cols] * vecs[slot, m, cols][None]
            if out is None:
                for m in range(3):
                    acc[m, rows] = sums[m]
            else:
                out[0, rows] = jnp.sum(sums[0] - sums[2], axis=1)
                out[1, rows] = jnp.sum(sums[0] + sums[1], axis=1)
            return 0

        lax.fori_loop(0, comp // SUB, body, 0)

    def finish_apply(out):
        put(0, fields[0, 0], fields[0, 1])
        products((8,), True, out)

    row16 = lax.broadcasted_iota(jnp.int32, (2 * SUB, lanes), 0)
    lane16 = lax.broadcasted_iota(jnp.int32, (2 * SUB, lanes), 1)

    def start_reduce(j, values):
        table = jnp.zeros((2 * SUB, lanes), jnp.float32)
        for k, value in enumerate(values):
            table = jnp.where(row16 == k, jnp.sum(value, axis=0, keepdims=True), table)
        table = jnp.sum(table, axis=1, keepdims=True)
        row = jnp.sum(jnp.where(row16 == lane16, table, 0.0), axis=0, keepdims=True)
        row_one[j] = row
        for k in range(1, n_xy):
            cp = remote(row_one.at[j], red_one.at[j, me_xy], one_send.at[j, k], one_recv.at[j, me_xy],
                        {"xy": lax.rem(me_xy + k, n_xy)})
            cp.start()
            pending.append(cp)
        red_one[j, me_xy] = row

    def middle_reduce(j):
        for k in range(1, n_xy):
            p = lax.rem(me_xy + n_xy - k, n_xy)
            remote(row_one.at[j], red_one.at[j, p], one_send.at[j, k], one_recv.at[j, p], {"xy": p}).wait_recv()
        row = red_one[j, 0]
        for k in range(1, n_xy):
            row = row + red_one[j, k]
        row_two[j] = row
        for k in range(1, n_two):
            cp = remote(row_two.at[j], red_two.at[j, me_two], two_send.at[j, k], two_recv.at[j, me_two], two_peer(k)[1])
            cp.start()
            pending.append(cp)
        red_two[j, me_two] = row

    def end_reduce(j, count):
        for k in range(1, n_two):
            p, device = two_peer(n_two - k)
            remote(row_two.at[j], red_two.at[j, p], two_send.at[j, k], two_recv.at[j, p], device).wait_recv()
        row = red_two[j, 0]
        for k in range(1, n_two):
            row = row + red_two[j, k]
        return [jnp.broadcast_to(row[:, k:k + 1], (1, lanes)) for k in range(count)]

    def load(ref):
        return (ref[0], ref[1])

    def store(ref, value):
        ref[0] = value[0]
        ref[1] = value[1]

    def dots(vector_refs, q):
        values = []
        for ref in vector_refs:
            values.extend(cmul_conj(load(ref), q))
        values.append(q[0] * q[0] + q[1] * q[1])
        return values

    waits = send_halo(0, src)
    for at, d in enumerate(ARRIVAL):
        if d == 6:
            set_y(src)
        elif d == 4:
            set_x(0, src, waits)
        elif d == 0:
            set_t(0, waits)
        elif d == 2:
            set_z(0, waits)
        loads[at].wait()
        convert(d)
        products((d,), at == 0, fields.at[0] if at == 7 else None)
    loads[8].wait()
    convert(8)
    raw = fields.at[1]
    finish_apply(raw)

    def apply(e, ref, out, j):
        set_y(ref)
        products((6, 7), True)
        middle_reduce(j)
        set_x(e, ref, waits)
        products((4, 5), False)
        set_t(e, waits)
        set_z(e, waits)
        products((0, 1, 2, 3), False, fields.at[0])
        finish_apply(out)

    source = load(src)
    q = load(raw)
    start_reduce(0, dots([src], q) + [source[0] * source[0] + source[1] * source[1]])
    waits = send_halo(1, raw)
    product = fields.at[2]
    apply(1, raw, product, 0)
    dot_re, dot_im, q_sq, norm_sq = end_reduce(0, 4)
    source_norm = jnp.sqrt(norm_sq)
    scale = 1.0 / source_norm
    store(vs.at[0], cscale(load(src), scale))
    store(qs.at[0], cscale(load(raw), scale))
    store(product, cscale(load(product), scale))
    g = [(dot_re * scale * scale, dot_im * scale * scale)]
    q_sq = q_sq * scale * scale

    columns = []
    low = [[None] * ITERS for _ in range(ITERS)]
    inv_diag, forward = [], []

    def factor_row(j):
        entries = []
        for k in range(j + 1):
            total = cmul_conj(columns[j][0], columns[k][0])
            for m in range(1, k + 2):
                term = cmul_conj(columns[j][m], columns[k][m])
                total = (total[0] + term[0], total[1] + term[1])
            entries.append(total)
        for k in range(j):
            total = entries[k]
            for m in range(k):
                total = csub(total, cmul_conj(low[k][m], low[j][m]))
            low[j][k] = cscale(total, inv_diag[k])
        diag = entries[j][0]
        for m in range(j):
            diag = diag - (low[j][m][0] * low[j][m][0] + low[j][m][1] * low[j][m][1])
        inv_diag.append(1.0 / jnp.sqrt(diag))
        total = (source_norm * columns[j][0][0], -source_norm * columns[j][0][1])
        for m in range(j):
            total = csub(total, cmul(low[j][m], forward[m]))
        forward.append(cscale(total, inv_diag[j]))

    zero = jnp.zeros((1, lanes), jnp.float32)
    for j in range(ITERS):
        length_sq = q_sq
        for re, im in g:
            length_sq = length_sq - (re * re + im * im)
        length = jnp.sqrt(length_sq)
        columns.append(g[:j] + [(g[j][0] + 1.0, g[j][1]), (length, zero)])
        if j < ITERS - 1:
            scale = 1.0 / length
            v = load(qs.at[j])
            q = load(product)
            for i in range(j + 1):
                v = csub(v, cmul(g[i], load(vs.at[i])))
                q = csub(q, cmul(g[i], load(qs.at[i])))
            store(qs.at[j + 1], cscale(q, scale))
            store(vs.at[j + 1], cscale(v, scale))
            last = j + 1 == ITERS - 1
            start_reduce(j + 1, dots([vs.at[i] for i in range(j + 2)], load(qs.at[j + 1])))
            if not last:
                waits = send_halo(j + 2, qs.at[j + 1])
            factor_row(j)
            if last:
                middle_reduce(j + 1)
            else:
                product = fields.at[j + 3]
                apply(j + 2, qs.at[j + 1], product, j + 1)
            got = end_reduce(j + 1, 2 * (j + 2) + 1)
            g = [(got[2 * i], got[2 * i + 1]) for i in range(j + 2)]
            q_sq = got[2 * (j + 2)]
        else:
            factor_row(j)

    coeffs = [None] * ITERS
    for j in reversed(range(ITERS)):
        total = forward[j]
        for m in range(j + 1, ITERS):
            total = csub(total, cmul_conj(low[m][j], coeffs[m]))
        coeffs[j] = cscale(total, inv_diag[j])

    answer = cmul(coeffs[0], load(vs.at[0]))
    left = csub(load(src), cmul(coeffs[0], load(qs.at[0])))
    for j in range(1, ITERS):
        term = cmul(coeffs[j], load(vs.at[j]))
        answer = (answer[0] + term[0], answer[1] + term[1])
        left = csub(left, cmul(coeffs[j], load(qs.at[j])))
    store(sol_ref, answer)
    store(res_ref, csub(left, answer))

    shape = hes_ref.shape[1:]
    part = lax.broadcasted_iota(jnp.int32, shape, 0)
    row = lax.broadcasted_iota(jnp.int32, shape, 1)
    for j in range(ITERS):
        table = jnp.zeros(shape, jnp.float32)
        for i in range(j + 2):
            re, im = (x[:, :shape[1]] for x in columns[j][i])
            table = jnp.where(row == i, jnp.where(part == 0, re, im), table)
        hes_ref[j] = table

    for cp in pending:
        cp.wait_send()


def hand_on(*refs):
    half = len(refs) // 2
    for i in range(half):
        refs[half + i][...] = refs[i][...]


def solution(mesh):
    sizes = tuple(mesh.shape[a] for a in ("ta", "gz", "xy"))

    def per_device(source, inverse, coarse_links):
        comp, lanes = source.shape[1], source.shape[4]
        f32 = jnp.float32
        field = (2, comp, lanes)
        mats = (9, comp, comp, lanes)
        n_two = sizes[0] * sizes[1]
        dma = pltpu.SemaphoreType.DMA
        hbm = pl.BlockSpec(memory_space=pl.ANY)
        vmem = pl.BlockSpec(memory_space=pltpu.VMEM)
        sol, res, hes = pl.pallas_call(
            functools.partial(kernel, sizes),
            out_shape=(
                jax.ShapeDtypeStruct(field, f32),
                jax.ShapeDtypeStruct(field, f32),
                jax.ShapeDtypeStruct((ITERS, 2, ITERS + 1), f32),
            ),
            in_specs=[hbm, hbm, hbm],
            out_specs=(vmem, vmem, vmem),
            scratch_shapes=[
                pltpu.VMEM((9, 2, comp, comp, lanes), coarse_links.dtype),
                pltpu.VMEM(mats, f32),
                pltpu.VMEM(mats, f32),
                pltpu.VMEM(mats, f32),
                pltpu.VMEM((8, 3, comp, lanes), f32),
                pltpu.VMEM((3, comp, SUB, lanes), f32),
                pltpu.VMEM(field, f32),
                pltpu.VMEM((ITERS + 1, *field), f32),
                pltpu.VMEM((ITERS, *field), f32),
                pltpu.VMEM((ITERS, *field), f32),
                pltpu.VMEM((ITERS, 2, *field), f32),
                pltpu.VMEM((ITERS, 2, *field), f32),
                pltpu.VMEM((ITERS, 2, 2, SUB, lanes), f32),
                pltpu.VMEM((ITERS, 2, 2, SUB, lanes), f32),
                pltpu.VMEM((ITERS, sizes[2], 1, lanes), f32),
                pltpu.VMEM((ITERS, n_two, 1, lanes), f32),
                pltpu.VMEM((ITERS, 1, lanes), f32),
                pltpu.VMEM((ITERS, 1, lanes), f32),
                dma((9,)),
                dma,
                dma((ITERS, 2)), dma((ITERS, 2)),
                dma((ITERS, 2)), dma((ITERS, 2)),
                dma((ITERS, 2)), dma((ITERS, 2)),
                dma((ITERS, sizes[2])), dma((ITERS, sizes[2])),
                dma((ITERS, n_two)), dma((ITERS, n_two)),
            ],
            compiler_params=pltpu.CompilerParams(
                collective_id=0, has_side_effects=True, vmem_limit_bytes=60 * 1024 * 1024),
        )(
            source.reshape(field),
            inverse.reshape(2, comp, comp, lanes),
            coarse_links.reshape(8, 2, comp, comp, lanes),
        )
        results = (sol, res, hes)
        sol, res, hes = pl.pallas_call(
            hand_on,
            out_shape=tuple(jax.ShapeDtypeStruct(x.shape, x.dtype) for x in results),
            in_specs=[vmem] * 3,
            out_specs=(vmem,) * 3,
        )(*results)
        return sol.reshape(source.shape), res.reshape(source.shape), hes.transpose(1, 2, 0)

    specs = (
        P(None, None, "ta", "gz", "xy"),
        P(None, None, None, "ta", "gz", "xy"),
        P(None, None, None, None, "ta", "gz", "xy"),
    )
    return jax.shard_map(
        per_device,
        mesh=mesh,
        in_specs=specs,
        out_specs=(specs[0], specs[0], P()),
        check_vma=False,
    )
```

profile of v0, /device:TPU:0, one launch (start us, length us, event | category | flops | bytes accessed | tf_op | source)
XLA Modules:
  0.0 52.3 jit_solution(9163087961424775248)
XLA Ops:
  0.6 50.2 %shard_map.58 = (f32[2,48,128]{2,1,0:T(8,128)}, f32[2,48,128]{2,1,0:T(8,128)}, f32[5,2,6]{2,1,0:T(2,128)}) custom-call(f32[2,48,128]{2,1,0:T(8,128)} %bitcast.12, bf16[2,48,48,128]{3,2,1,0:T(8,128)(2,1)} %bitcast.11, bf16[8,2,48,48,128]{4,3,2,1,0:T(8,128)(2,1)} %bitcast.10), custom_call_target="tpu_custom_call" | custom-call | tf_op jit(solution)/shard_map/pallas_call | solution.py:399
  50.8 1.5 %shard_map.59 = (f32[2,48,128]{2,1,0:T(8,128)}, f32[2,48,128]{2,1,0:T(8,128)}, f32[5,2,6]{2,1,0:T(2,128)}) custom-call(f32[2,48,128]{2,1,0:T(8,128)} %get-tuple-element.9.refs_0_, f32[2,48,128]{2,1,0:T(8,128)} %get-tuple-element.10.refs_1_, f32[5,2,6]{2,1,0:T(2,128)} %get-tuple-element.11.refs_2_), custom_call_target="tpu_custom_call" | custom-call | tf_op jit(solution)/shard_map/pallas_call | solution.py:443
where the time goes:
time: 52.5 us; the launch traced here: 52.3 us
  Pallas kernels  51.7 us (98%)
  between operations  0.64 us (1%)
    pallas_call x1, Pallas kernels, per_device(): pl.pallas_call(functools.partial(kernel, sizes), out_shape=(jax.ShapeDtyp...  50.2 us
    pallas_call x1, Pallas kernels, per_device(): pl.pallas_call(hand_on, out_shape=tuple((jax.ShapeDtypeStruct(x.shape, x....  1.47 us

commit v1 on v0

v1 whole, which is shorter than its diff:
```python
import functools

import jax
import jax.numpy as jnp
from jax import lax
from jax.experimental import pallas as pl
from jax.experimental.pallas import tpu as pltpu
from jax.sharding import PartitionSpec as P

LY = 16
ITERS = 5
SUB = 8
PARTS = 3
DOTS = 2 * ITERS + 1
MESH = pl.DeviceIdType.MESH
ARRIVAL = (6, 7, 4, 5, 0, 1, 2, 3)


def cmul(a, b):
    return (a[0] * b[0] - a[1] * b[1], a[0] * b[1] + a[1] * b[0])


def cmul_conj(a, b):
    return (a[0] * b[0] + a[1] * b[1], a[0] * b[1] - a[1] * b[0])


def cadd(a, b):
    if a is None:
        return b
    return (a[0] + b[0], a[1] + b[1])


def csub(a, b):
    if a is None:
        return (-b[0], -b[1])
    return (a[0] - b[0], a[1] - b[1])


def cscale(a, s):
    return (a[0] * s, a[1] * s)


def conj(a):
    return (a[0], -a[1])


def kernel(sizes, source_hbm, inverse_hbm, links_hbm, sol_ref, res_ref, hes_ref,
           stage, mat_a, mat_b, mat_s, vecs, acc, ys,
           halo_t, halo_z, halo_x, pack, red_one, red_two, red_all, row_one, row_two,
           load_sem, src_sem, t_send, t_recv, z_send, z_recv, x_send, x_recv,
           one_send, one_recv, two_send, two_recv, all_send, all_recv):
    n_ta, n_gz, n_xy = sizes
    comp, lanes = ys.shape[2], ys.shape[3]
    tiles = comp // SUB
    pitch = mat_a.shape[0] // (9 * comp)
    width = comp // PARTS
    me_ta, me_gz, me_xy = (lax.axis_index(a) for a in ("ta", "gz", "xy"))
    n_two = n_ta * n_gz
    n_all = n_two * n_xy
    me_two = me_ta * n_gz + me_gz
    me_all = me_two * n_xy + me_xy
    far = (me_gz + 1) // n_gz

    src = ys.at[0]
    pltpu.make_async_copy(source_hbm, src, src_sem).start()
    loads = []
    for d in ARRIVAL:
        loads.append(pltpu.make_async_copy(links_hbm.at[d], stage.at[d], load_sem.at[d]))
    loads.append(pltpu.make_async_copy(inverse_hbm, stage.at[8], load_sem.at[8]))
    for load in loads:
        load.start()

    def two_peer(k):
        p = lax.rem(me_two + k, n_two)
        return p, {"ta": p // n_gz, "gz": lax.rem(p, n_gz)}

    def all_peer(k):
        p = lax.rem(me_all + k, n_all)
        q = p // n_xy
        return {"ta": q // n_gz, "gz": lax.rem(q, n_gz), "xy": lax.rem(p, n_xy)}

    def step_to(axis, step):
        me, n = {"ta": (me_ta, n_ta), "gz": (me_gz, n_gz), "xy": (me_xy, n_xy)}[axis]
        return {axis: lax.rem(me + step + n, n)}

    barrier = pltpu.get_barrier_semaphore()
    greeted = [all_peer(k) for k in range(1, n_all)]
    for device in greeted:
        pl.semaphore_signal(barrier, inc=1, device_id=device, device_id_type=MESH)
    pltpu.make_async_copy(source_hbm, src, src_sem).wait()
    pl.semaphore_wait(barrier, len(greeted))

    lane = lax.broadcasted_iota(jnp.int32, (SUB, lanes), 1)
    lane_all = lax.broadcasted_iota(jnp.int32, (comp, lanes), 1)
    pending = []

    def remote(s, d, send, recv, device):
        return pltpu.make_async_remote_copy(
            src_ref=s, dst_ref=d, send_sem=send, recv_sem=recv, device_id=device, device_id_type=MESH)

    def go(copy):
        copy.start()
        pending.append(copy)

    def packed(value, first):
        out = jnp.zeros((SUB, lanes), jnp.float32)
        for k in range(tiles):
            tile = value[k * SUB:(k + 1) * SUB]
            shift = (LY * k + (0 if first else LY)) % lanes
            if shift:
                tile = pltpu.roll(tile, shift, 1)
            out = jnp.where(lane // LY == k, tile, out)
        return out

    def unpacked(value, first):
        out = []
        for k in range(tiles):
            shift = ((0 if first else lanes - LY) - LY * k) % lanes
            out.append(pltpu.roll(value, shift, 1) if shift else value)
        return jnp.concatenate(out, axis=0)

    def part(ref, p):
        return ref.at[:, pl.ds(p * width, width)]

    def z_copy(e, slot, p):
        step = 2 * slot - 1
        return remote(part(ys.at[e], p), part(halo_z.at[e, slot], p),
                      z_send.at[e, slot, p], z_recv.at[e, slot, p], step_to("gz", step))

    def t_copy(e, slot):
        return remote(ys.at[e], halo_t.at[e, slot], t_send.at[e, slot], t_recv.at[e, slot],
                      step_to("ta", 2 * slot - 1))

    def x_copy(e, slot):
        return remote(pack.at[e, slot], halo_x.at[e, slot], x_send.at[e, slot], x_recv.at[e, slot],
                      step_to("xy", 2 * slot - 1))

    def send_part(e, p):
        go(z_copy(e, far, p))
        go(z_copy(e, 1 - far, p))

    def send_rest(e):
        for slot in range(1 if n_ta == 2 else 2):
            go(t_copy(e, slot))
        for c in range(2):
            value = ys[e, c]
            pack[e, 0, c] = packed(value, True)
            pack[e, 1, c] = packed(value, False)
        for slot in range(2):
            go(x_copy(e, slot))

    def put(slot, re, im, rows=slice(None)):
        vecs[slot, 0, rows] = re
        vecs[slot, 1, rows] = im - re
        vecs[slot, 2, rows] = re + im

    def set_y(e):
        pos = lane_all % LY
        fwd, bwd = [], []
        for c in range(2):
            v = ys[e, c]
            fwd.append(jnp.where(pos == LY - 1, pltpu.roll(v, LY - 1, 1), pltpu.roll(v, lanes - 1, 1)))
            bwd.append(jnp.where(pos == 0, pltpu.roll(v, lanes - LY + 1, 1), pltpu.roll(v, 1, 1)))
        put(6, *fwd)
        put(7, *bwd)

    def set_x(e):
        fwd, bwd = [], []
        for slot in range(2):
            x_copy(e, slot).wait_recv()
        for c in range(2):
            v = ys[e, c]
            fwd.append(jnp.where(lane_all >= lanes - LY, unpacked(halo_x[e, 0, c], False), pltpu.roll(v, lanes - LY, 1)))
            bwd.append(jnp.where(lane_all < LY, unpacked(halo_x[e, 1, c], True), pltpu.roll(v, LY, 1)))
        put(4, *fwd)
        put(5, *bwd)

    def set_t(e):
        t_copy(e, 0).wait_recv()
        put(0, halo_t[e, 0, 0], halo_t[e, 0, 1])
        back = 0
        if n_ta != 2:
            t_copy(e, 1).wait_recv()
            back = 1
        put(1, halo_t[e, back, 0], halo_t[e, back, 1])

    def set_z(e, slot, vec, p):
        z_copy(e, slot, p).wait_recv()
        rows = pl.ds(p * width, width)
        put(vec, halo_z[e, slot, 0, rows], halo_z[e, slot, 1, rows], rows)

    def convert(d):
        def body(i, _):
            for row in range(2):
                at = i * 2 + row
                a = stage[d, 0, at].astype(jnp.float32)
                b = stage[d, 1, at].astype(jnp.float32)
                s = a + b
                for k in range(tiles):
                    where = pl.ds((d * comp + k * SUB) * pitch + at, SUB, stride=pitch)
                    cols = slice(k * SUB, (k + 1) * SUB)
                    mat_a[where] = a[cols]
                    mat_b[where] = b[cols]
                    mat_s[where] = s[cols]
            return 0

        lax.fori_loop(0, comp // 2, body, 0)

    mats = (mat_s, mat_a, mat_b)

    def sweep(d, vec, first, count, rows, start, unroll=SUB):
        def body(b, sums):
            sums = list(sums)
            for u in range(unroll):
                j = first + b * unroll + u
                base = (d * comp + j) * pitch
                for m in range(3):
                    x = vecs[vec, m, pl.ds(j, SUB, stride=0)]
                    for t, k in enumerate(rows):
                        sums[m * len(rows) + t] += mats[m][pl.ds(base + k * SUB, SUB)] * x
            return tuple(sums)

        return lax.fori_loop(0, count // unroll, body, tuple(start))

    every = range(tiles)

    def products(dirs, first=False):
        if first:
            sums = [jnp.zeros((SUB, lanes), jnp.float32)] * (3 * tiles)
        else:
            sums = [acc[m] for m in range(3 * tiles)]
        for d, vec, begin, count in dirs:
            sums = sweep(d, vec, begin, count, every, sums)
        for m in range(3 * tiles):
            acc[m] = sums[m]

    def whole(d, vec=None):
        return (d, d if vec is None else vec, 0, comp)

    def hop_done():
        for k in every:
            s, a, b = (acc[m * tiles + k] for m in range(3))
            put(8, s - b, s + a, pl.ds(k * SUB, SUB))

    def invert(e, coeffs, then):
        group = tiles // PARTS
        for p in range(PARTS):
            rows = range(p * group, (p + 1) * group)
            sums = sweep(8, 8, 0, comp, rows, [jnp.zeros((SUB, lanes), jnp.float32)] * (3 * group), 2 * SUB)
            for t, k in enumerate(rows):
                s, a, b = (sums[m * group + t] for m in range(3))
                y = (s - b, s + a)
                at = pl.ds(k * SUB, SUB)
                if coeffs is not None:
                    factor, others = coeffs
                    y = cscale(y, factor)
                    for l, u in enumerate(others):
                        if u is not None:
                            y = cadd(y, cmul(u, (ys[l, 0, at], ys[l, 1, at])))
                ys[e + 1, 0, at] = y[0]
                ys[e + 1, 1, at] = y[1]
            then(p)

    row16 = lax.broadcasted_iota(jnp.int32, (2 * SUB, lanes), 0)
    lane16 = lax.broadcasted_iota(jnp.int32, (2 * SUB, lanes), 1)

    def dots(pairs):
        values = []
        for l, i in pairs:
            re = im = None
            for k in every:
                at = pl.ds(k * SUB, SUB)
                r, m = cmul_conj((ys[l, 0, at], ys[l, 1, at]), (ys[i, 0, at], ys[i, 1, at]))
                re = r if re is None else re + r
                im = m if im is None else im + m
            values.append(re)
            if l != i:
                values.append(im)
        table = jnp.zeros((2 * SUB, lanes), jnp.float32)
        for k, value in enumerate(values):
            table = jnp.where(row16 == k, jnp.sum(value, axis=0, keepdims=True), table)
        table = jnp.sum(table, axis=1, keepdims=True)
        return jnp.sum(jnp.where(row16 == lane16, table, 0.0), axis=0, keepdims=True)

    def pairs_of(i):
        return [(l, i) for l in range(i + 1)]

    def start_reduce(j, row):
        row_one[j] = row
        for k in range(1, n_xy):
            go(remote(row_one.at[j], red_one.at[j, me_xy], one_send.at[j, k], one_recv.at[j, me_xy],
                      {"xy": lax.rem(me_xy + k, n_xy)}))
        red_one[j, me_xy] = row

    def middle_reduce(j):
        for k in range(1, n_xy):
            p = lax.rem(me_xy + n_xy - k, n_xy)
            remote(row_one.at[j], red_one.at[j, p], one_send.at[j, k], one_recv.at[j, p], {"xy": p}).wait_recv()
        row = red_one[j, 0]
        for k in range(1, n_xy):
            row = row + red_one[j, k]
        row_two[j] = row
        for k in range(1, n_two):
            go(remote(row_two.at[j], red_two.at[j, me_two], two_send.at[j, k], two_recv.at[j, me_two], two_peer(k)[1]))
        red_two[j, me_two] = row

    def spread(row, count):
        row = jnp.broadcast_to(row, (SUB, lanes))
        return [jnp.broadcast_to(row[:, k:k + 1], (SUB, lanes)) for k in range(count)]

    def end_reduce(j, count):
        for k in range(1, n_two):
            p, device = two_peer(n_two - k)
            remote(row_two.at[j], red_two.at[j, p], two_send.at[j, k], two_recv.at[j, p], device).wait_recv()
        row = red_two[j, 0]
        for k in range(1, n_two):
            row = row + red_two[j, k]
        return spread(row, count)

    last = ITERS - 1

    def all_copy(k):
        return remote(row_one.at[last], red_all.at[me_all], all_send, all_recv, all_peer(k))

    def start_all(row):
        row_one[last] = row
        for k in range(1, n_all):
            all_copy(k).start()
        red_all[me_all] = row

    def end_all(count):
        others = red_all.at[pl.ds(0, n_all - 1)]
        pltpu.make_async_copy(others, others, all_recv).wait()
        terms = [red_all[k] for k in range(n_all)]
        while len(terms) > 1:
            terms = [a + b for a, b in zip(terms[::2], terms[1::2])] + terms[len(terms) & ~1:]
        return spread(terms[0], count)

    n = ITERS + 1
    zero = jnp.zeros((SUB, lanes), jnp.float32)
    one = jnp.ones((SUB, lanes), jnp.float32)
    gram = [[None] * n for _ in range(n)]
    tri = [[None] * n for _ in range(n)]
    inv_tri = [None] * n
    rec = [[None] * ITERS for _ in range(n)]
    shifted = [[None] * ITERS for _ in range(n)]
    hess = [[None] * ITERS for _ in range(n)]

    def set_gram(i, values):
        for l in range(i):
            gram[l][i] = (values[2 * l], values[2 * l + 1])
            gram[i][l] = conj(gram[l][i])
        gram[i][i] = (values[2 * i], zero)
        for l in range(i):
            total = gram[l][i]
            for k in range(l):
                total = csub(total, cmul_conj(tri[k][l], tri[k][i]))
            tri[l][i] = cscale(total, inv_tri[l])
        total = values[2 * i]
        for k in range(i):
            total = total - (tri[k][i][0] * tri[k][i][0] + tri[k][i][1] * tri[k][i][1])
        root = jnp.sqrt(total)
        tri[i][i] = (root, zero)
        inv_tri[i] = 1.0 / root

    def set_rec(i, column):
        for l, value in enumerate(column):
            rec[l][i] = value
            shifted[l][i] = value
        shifted[i][i] = (one if rec[i][i] is None else rec[i][i][0] + 1.0, zero if rec[i][i] is None else rec[i][i][1])

    def next_coeffs(i):
        k = i - 1
        r = [None] * (k + 1)
        r[k] = (inv_tri[k], zero)
        for l in reversed(range(k)):
            total = None
            for m in range(l + 1, k + 1):
                term = cscale(tri[l][m], r[m][0]) if m == k else cmul(tri[l][m], r[m])
                total = csub(total, term)
            r[l] = cscale(total, inv_tri[l])
        t = [None] * (i + 1)
        for m in range(k + 1):
            for l in range(m + 2):
                if rec[l][m] is not None:
                    term = cscale(r[m], rec[l][m][0]) if l == m + 1 else cmul(rec[l][m], r[m])
                    t[l] = cadd(t[l], term)
        u = [None] * (i + 1)
        for m in range(i):
            if t[m] is not None:
                for l in range(m + 2):
                    if rec[l][m] is not None:
                        term = cscale(t[m], rec[l][m][0]) if l == m + 1 else cmul(rec[l][m], t[m])
                        u[l] = cadd(u[l], term)
        factor = t[i][0]
        back = 1.0 / factor
        column = [None if v is None else cscale(v, -back) for v in u] + [(back, zero)]
        set_rec(i, column)
        return factor, u

    def hess_column(j):
        for l in range(j + 2):
            total = None
            for m in range(max(l, 0), j + 2):
                if rec[m][j] is not None:
                    if m == j + 1:
                        term = cscale(tri[l][m], rec[m][j][0])
                    elif m == l:
                        term = cscale(rec[m][j], tri[l][m][0])
                    else:
                        term = cmul(tri[l][m], rec[m][j])
                    total = cadd(total, term)
            for k in range(max(l - 1, 0), j):
                total = csub(total, cmul(hess[l][k], tri[k][j]))
            hess[l][j] = cscale(total, inv_tri[j])

    low = [[None] * ITERS for _ in range(ITERS)]
    inv_low, forward = [], []

    def times(g, b, real):
        return cscale(g, b[0]) if real else cmul(g, b)

    def factor_row(j):
        def g_times(l):
            total = None
            for m in range(j + 2):
                if shifted[m][j] is not None:
                    total = cadd(total, times(gram[l][m], shifted[m][j], m == j + 1))
            return total

        image_j = [g_times(l) for l in range(j + 2)]
        entries = []
        for a in range(j + 1):
            total = None
            for l in range(a + 2):
                if shifted[l][a] is not None:
                    term = cscale(image_j[l], shifted[l][a][0]) if l == a + 1 else cmul_conj(shifted[l][a], image_j[l])
                    total = cadd(total, term)
            entries.append(conj(total))
        for k in range(j):
            total = entries[k]
            for m in range(k):
                total = csub(total, cmul_conj(low[k][m], low[j][m]))
            low[j][k] = cscale(total, inv_low[k])
        diag = entries[j][0]
        for m in range(j):
            diag = diag - (low[j][m][0] * low[j][m][0] + low[j][m][1] * low[j][m][1])
        inv_low.append(1.0 / jnp.sqrt(diag))
        total = None
        for l in range(j + 2):
            if shifted[l][j] is not None:
                term = cscale(gram[l][0], shifted[l][j][0]) if l == j + 1 else cmul_conj(shifted[l][j], gram[l][0])
                total = cadd(total, term)
        for m in range(j):
            total = csub(total, cmul(low[j][m], forward[m]))
        forward.append(cscale(total, inv_low[j]))

    set_rec(0, [None, (one, zero)])
    set_rec(1, [None, None, (one, zero)])
    set_rec(last, [None] * ITERS + [(one, zero)])

    for p in range(PARTS):
        send_part(0, p)
    send_rest(0)
    for e in range(ITERS):
        if e:
            start_reduce(e - 1, dots([(0, 0), (0, 1), (1, 1)] if e == 1 else pairs_of(e)))
            set_y(e)
            products([whole(6), whole(7)], True)
            set_x(e)
            products([whole(4), whole(5)])
            set_t(e)
            products([whole(0), whole(1)])
            middle_reduce(e - 1)
            for p in range(PARTS):
                set_z(e, far, 2, p)
            products([whole(2 + far, 2)])
        else:
            for at, d in enumerate(ARRIVAL[:6]):
                if d == 6:
                    set_y(0)
                elif d == 4:
                    set_x(0)
                elif d == 0:
                    set_t(0)
                loads[at].wait()
                convert(d)
                products([whole(d)], at == 0)
            for at in (6, 7, 8):
                loads[at].wait()
                convert((ARRIVAL + (8,))[at])
            for p in range(PARTS):
                set_z(0, far, 2, p)
            products([whole(2 + far, 2)])
        coeffs = None
        if e == 2:
            values = end_reduce(0, 4)
            set_gram(0, values[:1])
            set_gram(1, values[1:])
            coeffs = next_coeffs(2)
        elif e == 3:
            set_gram(2, end_reduce(1, 5))
            coeffs = next_coeffs(3)
        elif e == 4:
            set_gram(3, end_reduce(2, 7))
        for p in range(PARTS):
            set_z(e, 1 - far, 3, p)
            products([(3 - far, 3, p * width, width)])
        hop_done()
        if e < last:
            invert(e, coeffs, functools.partial(send_part, e + 1))
            send_rest(e + 1)
        else:
            invert(e, coeffs, lambda p: None)
    start_all(dots(pairs_of(ITERS)))

    for j in range(3):
        hess_column(j)
        factor_row(j)
    set_gram(4, end_reduce(3, 9))
    hess_column(3)
    factor_row(3)

    shape = hes_ref.shape[1:]
    part_at = lax.broadcasted_iota(jnp.int32, shape, 0)
    row_at = lax.broadcasted_iota(jnp.int32, shape, 1)

    def write_column(j):
        table = jnp.zeros(shape, jnp.float32)
        for i in range(j + 2):
            re, im = (x[:shape[0], :shape[1]] for x in hess[i][j])
            re = re + 1.0 if i == j else re
            table = jnp.where(row_at == i, jnp.where(part_at == 0, re, im), table)
        hes_ref[j] = table

    for j in range(last):
        write_column(j)

    set_gram(5, end_all(DOTS))
    factor_row(last)
    weights = [None] * ITERS
    for j in reversed(range(ITERS)):
        total = forward[j]
        for m in range(j + 1, ITERS):
            total = csub(total, cmul_conj(low[m][j], weights[m]))
        weights[j] = cscale(total, inv_low[j])
    outer = [None] * n
    for j in range(ITERS):
        for l in range(j + 2):
            if shifted[l][j] is not None:
                outer[l] = cadd(outer[l], times(weights[j], shifted[l][j], l == j + 1))
    for k in every:
        at = pl.ds(k * SUB, SUB)
        left = (ys[0, 0, at], ys[0, 1, at])
        answer = None
        for l in range(n):
            y = (ys[l, 0, at], ys[l, 1, at])
            if l < ITERS:
                answer = cadd(answer, cmul(weights[l], y))
            left = csub(left, cmul(outer[l], y))
        for c in range(2):
            sol_ref[c, at] = answer[c]
            res_ref[c, at] = left[c]
    hess_column(last)
    write_column(last)

    for cp in pending:
        cp.wait_send()
    others = red_all.at[pl.ds(0, n_all - 1)]
    pltpu.make_async_copy(others, others, all_send).wait()


def hand_on(*refs):
    half = len(refs) // 2
    for i in range(half):
        refs[half + i][...] = refs[i][...]


def solution(mesh):
    sizes = tuple(mesh.shape[a] for a in ("ta", "gz", "xy"))

    def per_device(source, inverse, coarse_links):
        comp, lanes = source.shape[1], source.shape[4]
        f32 = jnp.float32
        field = (2, comp, lanes)
        pitch = comp + 1
        mats = (9 * comp * pitch, lanes)
        n_two = sizes[0] * sizes[1]
        dma = pltpu.SemaphoreType.DMA
        hbm = pl.BlockSpec(memory_space=pl.ANY)
        vmem = pl.BlockSpec(memory_space=pltpu.VMEM)
        sol, res, hes = pl.pallas_call(
            functools.partial(kernel, sizes),
            out_shape=(
                jax.ShapeDtypeStruct(field, f32),
                jax.ShapeDtypeStruct(field, f32),
                jax.ShapeDtypeStruct((ITERS, 2, ITERS + 1), f32),
            ),
            in_specs=[hbm, hbm, hbm],
            out_specs=(vmem, vmem, vmem),
            scratch_shapes=[
                pltpu.VMEM((9, 2, comp, comp, lanes), coarse_links.dtype),
                pltpu.VMEM(mats, f32),
                pltpu.VMEM(mats, f32),
                pltpu.VMEM(mats, f32),
                pltpu.VMEM((9, 3, comp, lanes), f32),
                pltpu.VMEM((3 * comp // SUB, SUB, lanes), f32),
                pltpu.VMEM((ITERS + 1, *field), f32),
                pltpu.VMEM((ITERS, 2, *field), f32),
                pltpu.VMEM((ITERS, 2, *field), f32),
                pltpu.VMEM((ITERS, 2, 2, SUB, lanes), f32),
                pltpu.VMEM((ITERS, 2, 2, SUB, lanes), f32),
                pltpu.VMEM((ITERS - 1, sizes[2], 1, lanes), f32),
                pltpu.VMEM((ITERS - 1, n_two, 1, lanes), f32),
                pltpu.VMEM((n_two * sizes[2], 1, lanes), f32),
                pltpu.VMEM((ITERS, 1, lanes), f32),
                pltpu.VMEM((ITERS - 1, 1, lanes), f32),
                dma((9,)),
                dma,
                dma((ITERS, 2)), dma((ITERS, 2)),
                dma((ITERS, 2, PARTS)), dma((ITERS, 2, PARTS)),
                dma((ITERS, 2)), dma((ITERS, 2)),
                dma((ITERS - 1, sizes[2])), dma((ITERS - 1, sizes[2])),
                dma((ITERS - 1, n_two)), dma((ITERS - 1, n_two)),
                dma, dma,
            ],
            compiler_params=pltpu.CompilerParams(
                collective_id=0, has_side_effects=True, vmem_limit_bytes=62 * 1024 * 1024),
        )(
            source.reshape(field),
            inverse.reshape(2, comp, comp, lanes),
            coarse_links.reshape(8, 2, comp, comp, lanes),
        )
        results = (sol, res, hes)
        sol, res, hes = pl.pallas_call(
            hand_on,
            out_shape=tuple(jax.ShapeDtypeStruct(x.shape, x.dtype) for x in results),
            in_specs=[vmem] * 3,
            out_specs=(vmem,) * 3,
        )(*results)
        return sol.reshape(source.shape), res.reshape(source.shape), hes.transpose(1, 2, 0)

    specs = (
        P(None, None, "ta", "gz", "xy"),
        P(None, None, None, "ta", "gz", "xy"),
        P(None, None, None, None, "ta", "gz", "xy"),
    )
    return jax.shard_map(
        per_device,
        mesh=mesh,
        in_specs=specs,
        out_specs=(specs[0], specs[0], P()),
        check_vma=False,
    )
```

time: 52.5 us -> 44.3 us (0.84)
  Pallas kernels: 51.7 us -> 43.5 us
    pallas_call x1, Pallas kernels: 50.2 us -> 42.1 us  [per_device(): pl.pallas_call(functools.partial(kernel, sizes), out_shape=(jax.ShapeDtyp...]
where the time goes in v1:
time: 44.3 us; the launch traced here: 44.2 us
  Pallas kernels  43.5 us (98%)
  between operations  0.64 us (1%)
    pallas_call x1, Pallas kernels, per_device(): pl.pallas_call(functools.partial(kernel, sizes), out_shape=(jax.ShapeDtyp...  42.1 us
    pallas_call x1, Pallas kernels, per_device(): pl.pallas_call(hand_on, out_shape=tuple((jax.ShapeDtypeStruct(x.shape, x....  1.47 us

profile of v1, /device:TPU:0, one launch (start us, length us, event | category | flops | bytes accessed | tf_op | source)
XLA Modules:
  0.0 44.2 jit_solution(3054506814013651865)
XLA Ops:
  0.6 42.1 %shard_map.58 = (f32[2,48,128]{2,1,0:T(8,128)}, f32[2,48,128]{2,1,0:T(8,128)}, f32[5,2,6]{2,1,0:T(2,128)}) custom-call(f32[2,48,128]{2,1,0:T(8,128)} %bitcast.12, bf16[2,48,48,128]{3,2,1,0:T(8,128)(2,1)} %bitcast.11, bf16[8,2,48,48,128]{4,3,2,1,0:T(8,128)(2,1)} %bitcast.10), custom_call_target="tpu_custom_call" | custom-call | tf_op jit(solution)/shard_map/pallas_call | solution.py:592
  42.7 1.5 %shard_map.59 = (f32[2,48,128]{2,1,0:T(8,128)}, f32[2,48,128]{2,1,0:T(8,128)}, f32[5,2,6]{2,1,0:T(2,128)}) custom-call(f32[2,48,128]{2,1,0:T(8,128)} %get-tuple-element.9.refs_0_, f32[2,48,128]{2,1,0:T(8,128)} %get-tuple-element.10.refs_1_, f32[5,2,6]{2,1,0:T(2,128)} %get-tuple-element.11.refs_2_), custom_call_target="tpu_custom_call" | custom-call | tf_op jit(solution)/shard_map/pallas_call | solution.py:635

commit v2 on v1

--- a/solution.py
+++ b/solution.py
@@ -13,7 +13,7 @@
 PARTS = 3
 DOTS = 2 * ITERS + 1
 MESH = pl.DeviceIdType.MESH
-ARRIVAL = (6, 7, 4, 5, 0, 1, 2, 3)
+ARRIVAL = (6, 7, 2, 3, 8, 4, 5, 0, 1)
 
 
 def cmul(a, b):
@@ -45,7 +45,7 @@
 
 
 def kernel(sizes, source_hbm, inverse_hbm, links_hbm, sol_ref, res_ref, hes_ref,
-           stage, mat_a, mat_b, mat_s, vecs, acc, ys,
+           stage, mat_a, mat_b, mat_s, vecs, acc, early, ys,
            halo_t, halo_z, halo_x, pack, red_one, red_two, red_all, row_one, row_two,
            load_sem, src_sem, t_send, t_recv, z_send, z_recv, x_send, x_recv,
            one_send, one_recv, two_send, two_recv, all_send, all_recv):
@@ -63,12 +63,11 @@
 
     src = ys.at[0]
     pltpu.make_async_copy(source_hbm, src, src_sem).start()
-    loads = []
+    loads = {}
     for d in ARRIVAL:
-        loads.append(pltpu.make_async_copy(links_hbm.at[d], stage.at[d], load_sem.at[d]))
-    loads.append(pltpu.make_async_copy(inverse_hbm, stage.at[8], load_sem.at[8]))
-    for load in loads:
-        load.start()
+        block = inverse_hbm if d == 8 else links_hbm.at[d]
+        loads[d] = pltpu.make_async_copy(block, stage.at[d], load_sem.at[d])
+        loads[d].start()
 
     def two_peer(k):
         p = lax.rem(me_two + k, n_two)
@@ -84,7 +83,11 @@
         return {axis: lax.rem(me + step + n, n)}
 
     barrier = pltpu.get_barrier_semaphore()
-    greeted = [all_peer(k) for k in range(1, n_all)]
+    if n_xy // 2 <= 2 and n_ta // 2 + n_gz // 2 <= 3:
+        greeted = [step_to(axis, step) for axis, size in (("xy", n_xy), ("gz", n_gz), ("ta", n_ta))
+                   for step in ((1, -1) if size > 2 else (1,))]
+    else:
+        greeted = [all_peer(k) for k in range(1, n_all)]
     for device in greeted:
         pl.semaphore_signal(barrier, inc=1, device_id=device, device_id_type=MESH)
     pltpu.make_async_copy(source_hbm, src, src_sem).wait()
@@ -164,47 +167,97 @@
         put(6, *fwd)
         put(7, *bwd)
 
-    def set_x(e):
-        fwd, bwd = [], []
+    def set_x_early(e):
+        sides = []
+        for c in range(2):
+            v = ys[e, c]
+            sides.append(jnp.where(lane_all < lanes - LY, pltpu.roll(v, lanes - LY, 1), pltpu.roll(v, LY, 1)))
+        put(4, *sides)
+
+    def set_x_late(e):
         for slot in range(2):
             x_copy(e, slot).wait_recv()
+        sides = []
         for c in range(2):
-            v = ys[e, c]
-            fwd.append(jnp.where(lane_all >= lanes - LY, unpacked(halo_x[e, 0, c], False), pltpu.roll(v, lanes - LY, 1)))
-            bwd.append(jnp.where(lane_all < LY, unpacked(halo_x[e, 1, c], True), pltpu.roll(v, LY, 1)))
-        put(4, *fwd)
-        put(5, *bwd)
+            side = jnp.where(lane_all < LY, unpacked(halo_x[e, 1, c], True), pltpu.roll(ys[e, c], LY, 1))
+            sides.append(jnp.where(lane_all < lanes - LY, side, unpacked(halo_x[e, 0, c], False)))
+        put(5, *sides)
 
     def set_t(e):
         t_copy(e, 0).wait_recv()
         put(0, halo_t[e, 0, 0], halo_t[e, 0, 1])
-        back = 0
         if n_ta != 2:
             t_copy(e, 1).wait_recv()
-            back = 1
-        put(1, halo_t[e, back, 0], halo_t[e, back, 1])
+            put(1, halo_t[e, 1, 0], halo_t[e, 1, 1])
 
     def set_z(e, slot, vec, p):
         z_copy(e, slot, p).wait_recv()
         rows = pl.ds(p * width, width)
         put(vec, halo_z[e, slot, 0, rows], halo_z[e, slot, 1, rows], rows)
 
+    def keep(d, at, a, b, s):
+        for k in range(tiles):
+            where = pl.ds((d * comp + k * SUB) * pitch + at, SUB, stride=pitch)
+            cols = slice(k * SUB, (k + 1) * SUB)
+            mat_a[where] = a[cols]
+            mat_b[where] = b[cols]
+            mat_s[where] = s[cols]
+
+    def widened(d, at):
+        return [stage[d, c, at].astype(jnp.float32) for c in range(2)]
+
     def convert(d):
+        loads[d].wait()
+
         def body(i, _):
-            for row in range(2):
-                at = i * 2 + row
-                a = stage[d, 0, at].astype(jnp.float32)
-                b = stage[d, 1, at].astype(jnp.float32)
-                s = a + b
-                for k in range(tiles):
-                    where = pl.ds((d * comp + k * SUB) * pitch + at, SUB, stride=pitch)
-                    cols = slice(k * SUB, (k + 1) * SUB)
-                    mat_a[where] = a[cols]
-                    mat_b[where] = b[cols]
-                    mat_s[where] = s[cols]
+            for u in range(2):
+                at = i * 2 + u
+                a, b = widened(d, at)
+                keep(d, at, a, b, a + b)
             return 0
 
         lax.fori_loop(0, comp // 2, body, 0)
+
+    def absorb(dirs, mix, first=False):
+        for d in dirs:
+            loads[d].wait()
+
+        def body(i, _):
+            for u in range(2):
+                at = i * 2 + u
+                sums = [None if first else early[m, at] for m in range(3)]
+                for d, (a, b) in mix([widened(d, at) for d in dirs]):
+                    s = a + b
+                    keep(d, at, a, b, s)
+                    for m, x in enumerate((s, a, b)):
+                        for k in range(tiles):
+                            cols = slice(k * SUB, (k + 1) * SUB)
+                            term = x[cols] * vecs[d, m, cols]
+                            sums[m] = term if sums[m] is None else sums[m] + term
+                for m in range(3):
+                    early[m, at] = sums[m]
+            return 0
+
+        lax.fori_loop(0, comp // 2, body, 0)
+
+    def plain(*dirs):
+        return lambda pairs: list(zip(dirs, pairs))
+
+    def mix_x(pairs):
+        low_side = lane_all < lanes - LY
+        return [(4, [jnp.where(low_side, f, b) for f, b in zip(*pairs)]),
+                (5, [jnp.where(low_side, b, f) for f, b in zip(*pairs)])]
+
+    def mix_t(pairs):
+        return [(0, [f + b for f, b in zip(*pairs)])]
+
+    def fold_early():
+        for k in range(tiles):
+            rows = slice(k * SUB, (k + 1) * SUB)
+            s, a, b = (early[m, rows] for m in range(3))
+            acc[k] = jnp.zeros((SUB, lanes), jnp.float32)
+            acc[tiles + k] = jnp.sum(s + a, axis=1)
+            acc[2 * tiles + k] = jnp.sum(b - s, axis=1)
 
     mats = (mat_s, mat_a, mat_b)
 
@@ -246,7 +299,7 @@
         group = tiles // PARTS
         for p in range(PARTS):
             rows = range(p * group, (p + 1) * group)
-            sums = sweep(8, 8, 0, comp, rows, [jnp.zeros((SUB, lanes), jnp.float32)] * (3 * group), 2 * SUB)
+            sums = sweep(8, 8, 0, comp, rows, [jnp.zeros((SUB, lanes), jnp.float32)] * (3 * group), comp)
             for t, k in enumerate(rows):
                 s, a, b = (sums[m * group + t] for m in range(3))
                 y = (s - b, s + a)
@@ -462,36 +515,36 @@
     for p in range(PARTS):
         send_part(0, p)
     send_rest(0)
+    t_dirs = (0,) if n_ta == 2 else (0, 1)
     for e in range(ITERS):
         if e:
             start_reduce(e - 1, dots([(0, 0), (0, 1), (1, 1)] if e == 1 else pairs_of(e)))
             set_y(e)
-            products([whole(6), whole(7)], True)
-            set_x(e)
-            products([whole(4), whole(5)])
+            set_x_early(e)
+            products([whole(6), whole(7), whole(4)], True)
+            if e > 1:
+                middle_reduce(e - 1)
+            set_x_late(e)
+            products([whole(5)])
             set_t(e)
-            products([whole(0), whole(1)])
-            middle_reduce(e - 1)
-            for p in range(PARTS):
-                set_z(e, far, 2, p)
-            products([whole(2 + far, 2)])
+            products([whole(d) for d in t_dirs])
+            if e == 1:
+                middle_reduce(0)
         else:
-            for at, d in enumerate(ARRIVAL[:6]):
-                if d == 6:
-                    set_y(0)
-                elif d == 4:
-                    set_x(0)
-                elif d == 0:
-                    set_t(0)
-                loads[at].wait()
+            set_y(0)
+            set_x_early(0)
+            absorb((6,), plain(6), True)
+            absorb((7,), plain(7))
+            for d in (2, 3, 8):
                 convert(d)
-                products([whole(d)], at == 0)
-            for at in (6, 7, 8):
-                loads[at].wait()
-                convert((ARRIVAL + (8,))[at])
-            for p in range(PARTS):
-                set_z(0, far, 2, p)
-            products([whole(2 + far, 2)])
+            set_x_late(0)
+            absorb((4, 5), mix_x)
+            set_t(0)
+            absorb((0, 1), mix_t if n_ta == 2 else plain(0, 1))
+            fold_early()
+        for p in range(PARTS):
+            set_z(e, far, 2, p)
+        products([whole(2 + far, 2)])
         coeffs = None
         if e == 2:
             values = end_reduce(0, 4)
@@ -605,6 +658,7 @@
                 pltpu.VMEM(mats, f32),
                 pltpu.VMEM((9, 3, comp, lanes), f32),
                 pltpu.VMEM((3 * comp // SUB, SUB, lanes), f32),
+                pltpu.VMEM((3, comp, SUB, lanes), f32),
                 pltpu.VMEM((ITERS + 1, *field), f32),
                 pltpu.VMEM((ITERS, 2, *field), f32),
                 pltpu.VMEM((ITERS, 2, *field), f32),

time: 44.3 us -> 41.7 us (0.941)
  Pallas kernels: 43.5 us -> 40.9 us
    pallas_call x1, Pallas kernels: 42.1 us -> 39.4 us  [per_device(): pl.pallas_call(functools.partial(kernel, sizes), out_shape=(jax.ShapeDtyp...]
where the time goes in v2:
time: 41.7 us; the launch traced here: 41.5 us
  Pallas kernels  40.9 us (98%)
  between operations  0.64 us (2%)
    pallas_call x1, Pallas kernels, per_device(): pl.pallas_call(functools.partial(kernel, sizes), out_shape=(jax.ShapeDtyp...  39.4 us
    pallas_call x1, Pallas kernels, per_device(): pl.pallas_call(hand_on, out_shape=tuple((jax.ShapeDtypeStruct(x.shape, x....  1.47 us

profile of v2, /device:TPU:0, one launch (start us, length us, event | category | flops | bytes accessed | tf_op | source)
XLA Modules:
  0.0 41.5 jit_solution(2546958566161098299)
XLA Ops:
  0.6 39.4 %shard_map.58 = (f32[2,48,128]{2,1,0:T(8,128)}, f32[2,48,128]{2,1,0:T(8,128)}, f32[5,2,6]{2,1,0:T(2,128)}) custom-call(f32[2,48,128]{2,1,0:T(8,128)} %bitcast.12, bf16[2,48,48,128]{3,2,1,0:T(8,128)(2,1)} %bitcast.11, bf16[8,2,48,48,128]{4,3,2,1,0:T(8,128)(2,1)} %bitcast.10), custom_call_target="tpu_custom_call" | custom-call | tf_op jit(solution)/shard_map/pallas_call | solution.py:645
  40.1 1.5 %shard_map.59 = (f32[2,48,128]{2,1,0:T(8,128)}, f32[2,48,128]{2,1,0:T(8,128)}, f32[5,2,6]{2,1,0:T(2,128)}) custom-call(f32[2,48,128]{2,1,0:T(8,128)} %get-tuple-element.9.refs_0_, f32[2,48,128]{2,1,0:T(8,128)} %get-tuple-element.10.refs_1_, f32[5,2,6]{2,1,0:T(2,128)} %get-tuple-element.11.refs_2_), custom_call_target="tpu_custom_call" | custom-call | tf_op jit(solution)/shard_map/pallas_call | solution.py:689

commit v3 on v2

--- a/solution.py
+++ b/solution.py
@@ -195,6 +195,11 @@
         rows = pl.ds(p * width, width)
         put(vec, halo_z[e, slot, 0, rows], halo_z[e, slot, 1, rows], rows)
 
+    def total_of(terms):
+        while len(terms) > 1:
+            terms = [a + b for a, b in zip(terms[::2], terms[1::2])] + terms[len(terms) & ~1:]
+        return terms[0]
+
     def keep(d, at, a, b, s):
         for k in range(tiles):
             where = pl.ds((d * comp + k * SUB) * pitch + at, SUB, stride=pitch)
@@ -223,22 +228,21 @@
             loads[d].wait()
 
         def body(i, _):
-            for u in range(2):
-                at = i * 2 + u
-                sums = [None if first else early[m, at] for m in range(3)]
+            for u in range(SUB):
+                at = i * SUB + u
+                terms = [[] if first else [early[m, at]] for m in range(3)]
                 for d, (a, b) in mix([widened(d, at) for d in dirs]):
                     s = a + b
                     keep(d, at, a, b, s)
                     for m, x in enumerate((s, a, b)):
                         for k in range(tiles):
                             cols = slice(k * SUB, (k + 1) * SUB)
-                            term = x[cols] * vecs[d, m, cols]
-                            sums[m] = term if sums[m] is None else sums[m] + term
+                            terms[m].append(x[cols] * vecs[d, m, cols])
                 for m in range(3):
-                    early[m, at] = sums[m]
+                    early[m, at] = total_of(terms[m])
             return 0
 
-        lax.fori_loop(0, comp // 2, body, 0)
+        lax.fori_loop(0, comp // SUB, body, 0)
 
     def plain(*dirs):
         return lambda pairs: list(zip(dirs, pairs))
@@ -589,6 +593,8 @@
     for j in range(last):
         write_column(j)
 
+    for cp in pending:
+        cp.wait_send()
     set_gram(5, end_all(DOTS))
     factor_row(last)
     weights = [None] * ITERS
@@ -617,8 +623,6 @@
     hess_column(last)
     write_column(last)
 
-    for cp in pending:
-        cp.wait_send()
     others = red_all.at[pl.ds(0, n_all - 1)]
     pltpu.make_async_copy(others, others, all_send).wait()
 
@@ -645,9 +649,9 @@
         sol, res, hes = pl.pallas_call(
             functools.partial(kernel, sizes),
             out_shape=(
-                jax.ShapeDtypeStruct(field, f32),
-                jax.ShapeDtypeStruct(field, f32),
-                jax.ShapeDtypeStruct((ITERS, 2, ITERS + 1), f32),
+                pltpu.VMEM(field, f32),
+                pltpu.VMEM(field, f32),
+                pltpu.VMEM((ITERS, 2, ITERS + 1), f32),
             ),
             in_specs=[hbm, hbm, hbm],
             out_specs=(vmem, vmem, vmem),
@@ -691,7 +695,7 @@
             out_shape=tuple(jax.ShapeDtypeStruct(x.shape, x.dtype) for x in results),
             in_specs=[vmem] * 3,
             out_specs=(vmem,) * 3,
-        )(*results)
+        )(*(pltpu.with_memory_space_constraint(x, pltpu.VMEM) for x in results))
         return sol.reshape(source.shape), res.reshape(source.shape), hes.transpose(1, 2, 0)
 
     specs = (

time: 41.7 us -> 39.8 us (0.954)
  Pallas kernels: 40.9 us -> 39 us
    pallas_call x1, Pallas kernels: 39.4 us -> 38.4 us  [per_device(): pl.pallas_call(functools.partial(kernel, sizes), out_shape=(pltpu.VMEM(fi...]
    pallas_call x1, Pallas kernels: 1.47 us -> 0.65 us  [per_device(): pl.pallas_call(hand_on, out_shape=tuple((jax.ShapeDtypeStruct(x.shape, x....]
where the time goes in v3:
time: 39.8 us; the launch traced here: 39.7 us
  Pallas kernels  39 us (98%)
  between operations  0.64 us (2%)
    pallas_call x1, Pallas kernels, per_device(): pl.pallas_call(functools.partial(kernel, sizes), out_shape=(pltpu.VMEM(fi...  38.4 us

profile of v3, /device:TPU:0, one launch (start us, length us, event | category | flops | bytes accessed | tf_op | source)
XLA Modules:
  0.0 39.7 jit_solution(9039855384670902422)
XLA Ops:
  0.6 38.4 %shard_map.58 = (f32[2,48,128]{2,1,0:T(8,128)S(1)}, f32[2,48,128]{2,1,0:T(8,128)S(1)}, f32[5,2,6]{2,1,0:T(2,128)S(1)}) custom-call(f32[2,48,128]{2,1,0:T(8,128)} %bitcast.12, bf16[2,48,48,128]{3,2,1,0:T(8,128)(2,1)} %bitcast.11, bf16[8,2,48,48,128]{4,3,2,1,0:T(8,128)(2,1)} %bitcast.10), custom_call_target="tpu_custom_call" | custom-call | tf_op jit(solution)/shard_map/pallas_call | solution.py:649
  39.0 0.6 %shard_map.59 = (f32[2,48,128]{2,1,0:T(8,128)}, f32[2,48,128]{2,1,0:T(8,128)}, f32[5,2,6]{2,1,0:T(2,128)}) custom-call(f32[2,48,128]{2,1,0:T(8,128)S(1)} %get-tuple-element.9.refs_0_, f32[2,48,128]{2,1,0:T(8,128)S(1)} %get-tuple-element.10.refs_1_, f32[5,2,6]{2,1,0:T(2,128)S(1)} %get-tuple-element.11.refs_2_), custom_call_target="tpu_custom_call" | custom-call | tf_op jit(solution)/shard_map/pallas_call | solution.py:693
